TPU v7x, 32 devices: a whole 2x2x4 slice. The times are simulated.
32 devices in a mesh: lat: 8 (over z, y), lon: 4 (over x, core).
Axes of the slice: x: 2, y: 2, z: 4, core: 2. Of those that a mesh axis runs over, the one named last changes fastest.
Arguments:
- field: bfloat16 [150, 128, 1024], P(None, 'lat', 'lon'), may hold values from -6 to 6
- land_mask: int32 [128, 1024], P('lat', 'lon'), may hold values 0 or 1
- fold_partner: int32 [1024], replicated, may hold values from 0 to 1023, as said below
- dw_kernel: float32 [150, 7, 7], replicated, may hold values from -0.875 to 0.875
- norm_gain: float32 [150], replicated, may hold values from 0.1 to 1.9
- w_in: bfloat16 [150, 600], replicated, may hold values from -0.5 to 0.5
- w_out: bfloat16 [600, 150], replicated, may hold values from -0.25 to 0.25
- spec_gain: float32 [2, 150, 512], replicated, may hold values from -12 to 12
- mix_weight: bfloat16 [150, 150], replicated, may hold values from -0.5 to 0.5
Outputs:
- block_out: bfloat16 [150, 128, 1024], P(None, 'lat', 'lon')
Inputs may be any that keep to these rules, and one draw needn't show every extreme that they name: There is one s such that fold_partner[j] = (s - j) mod 1024 for every j.
All inputs are finite; a program needn't handle non-finite values. No bound on the sum of `land_mask` on one device may be relied on, other than what follows from the above.
Results may differ from a plain program's by a relative error of at most 0.0065.
Values may be sent and summed in bfloat16 or wider, within the bound.
A program may use at most 128 MiB of HBM per device.

v0:
```python
import math
import jax
import jax.numpy as jnp
from jax import lax
from jax.sharding import PartitionSpec as P


def extended_2(cells, sides, width, closed):
    for axis, dim in sides:
        count = lax.axis_size(axis)
        ends = count if closed else count - 1
        head = lax.slice_in_dim(cells, 0, width, axis=dim)
        tail = lax.slice_in_dim(cells, cells.shape[dim] - width, cells.shape[dim], axis=dim)
        cells = jnp.concatenate(
            [
                lax.ppermute(tail, axis, [(i, (i + 1) % count) for i in range(ends)]),
                cells,
                lax.ppermute(head, axis, [((i + 1) % count, i) for i in range(ends)]),
            ],
            axis=dim,
        )
    return cells


def dft_table(lon_points, mode_count, col_count):
    points = jnp.arange(col_count, dtype=jnp.int32)
    freqs = jnp.arange(mode_count, dtype=jnp.int32)
    phase_index = points[:, None] * freqs[None, :] % lon_points
    angles = phase_index.astype(jnp.float32) * (2.0 * math.pi / lon_points)
    factor = 1.0 / math.sqrt(lon_points)
    return jnp.concatenate([jnp.cos(angles) * factor, -jnp.sin(angles) * factor], axis=1).astype(
        jnp.bfloat16
    )


def apply_gain(spectrum, spec_gain, mode_count):
    spec_re = spectrum[..., :mode_count]
    spec_im = spectrum[..., mode_count:]
    gain_re = spec_gain[0][:, None, :]
    gain_im = spec_gain[1][:, None, :]
    return jnp.concatenate(
        [gain_re * spec_re - gain_im * spec_im, gain_re * spec_im + gain_im * spec_re], axis=-1
    ).astype(jnp.bfloat16)


def depthwise_conv(extended, dw_kernel, lat_rows, lon_cols):
    total = jnp.zeros((extended.shape[0], lat_rows, lon_cols), jnp.float32)
    for tap_row in range(7):
        for tap_col in range(7):
            weight_col = dw_kernel[:, tap_row, tap_col][:, None, None]
            total = total + weight_col * extended[
                :, tap_row : tap_row + lat_rows, tap_col : tap_col + lon_cols
            ].astype(jnp.float32)
    return total


def point_mixer(depth, masked, wet_grid, norm_gain, w_in, w_out):
    channels = depth.shape[0]
    flat = depth.reshape(channels, -1)
    average = jnp.mean(flat, axis=0, keepdims=True)
    centred = flat - average
    variance = jnp.mean(centred * centred, axis=0, keepdims=True)
    normed = (centred * lax.rsqrt(variance + 1e-06) * norm_gain[:, None]).astype(jnp.bfloat16)
    pre_act = jnp.einsum("ch,cp->hp", w_in, normed, preferred_element_type=jnp.float32)
    hidden = jax.nn.gelu(pre_act, approximate=True).astype(jnp.bfloat16)
    branch = jnp.einsum("hc,hp->cp", w_out, hidden, preferred_element_type=jnp.float32)
    wet_flat = wet_grid.reshape(1, -1).astype(jnp.float32)
    result = wet_flat * (masked.reshape(channels, -1).astype(jnp.float32) + branch)
    return result.astype(jnp.bfloat16).reshape(depth.shape)


def local(field, land_mask, fold_partner, dw_kernel, norm_gain, w_in, w_out, spec_gain, mix_weight):
    channels, lat_rows, lon_cols = field.shape
    lat_count = lax.axis_size("lat")
    lon_count = lax.axis_size("lon")
    lon_points = lon_cols * lon_count
    mode_count = spec_gain.shape[2]
    wet_grid = land_mask.astype(field.dtype)
    masked = field * wet_grid[None]
    top_rows = masked[:, lat_rows - 3 :, :][:, ::-1, :]
    fold_full = lax.all_gather(top_rows, "lon", axis=2, tiled=True)
    lon_first = lax.axis_index("lon") * lon_cols
    window = (lon_first - 3 + jnp.arange(lon_cols + 6, dtype=jnp.int32)) % lon_points
    ghost_rows = jnp.take(fold_full, jnp.take(fold_partner, window), axis=2)
    lat_index = lax.axis_index("lat")
    lon_padded = extended_2(masked, (("lon", 2),), 3, True)
    padded = extended_2(lon_padded, (("lat", 1),), 3, False)
    south_rows = padded[:, :3]
    north_rows = jnp.where(lat_index == lat_count - 1, ghost_rows, padded[:, lat_rows + 3 :])
    extended = jnp.concatenate([south_rows, padded[:, 3 : lat_rows + 3], north_rows], axis=1)
    depth = depthwise_conv(extended, dw_kernel, lat_rows, lon_cols)
    group_rows = math.gcd(lat_rows, 8)

    def mix_rows(group_index, result):
        offset = group_index * group_rows
        mixed_block = point_mixer(
            lax.dynamic_slice_in_dim(depth, offset, group_rows, 1),
            lax.dynamic_slice_in_dim(masked, offset, group_rows, 1),
            lax.dynamic_slice_in_dim(wet_grid, offset, group_rows, 0),
            norm_gain,
            w_in,
            w_out,
        )
        return lax.dynamic_update_slice_in_dim(result, mixed_block, offset, 1)

    residual = lax.fori_loop(
        0, lat_rows // group_rows, mix_rows, jnp.zeros(field.shape, jnp.bfloat16)
    )
    by_rows = lax.all_to_all(residual, "lon", split_axis=1, concat_axis=2, tiled=True)
    row_count = by_rows.shape[1]
    fourier = dft_table(lon_points, mode_count, lon_points)
    spectrum = jnp.dot(
        by_rows.reshape(channels * row_count, lon_points),
        fourier,
        preferred_element_type=jnp.float32,
    )
    scaled = apply_gain(
        spectrum.reshape(channels, row_count, 2 * mode_count), spec_gain, mode_count
    )
    along_rows = jnp.einsum(
        "crk,nk->crn", scaled, fourier, preferred_element_type=jnp.float32
    ).astype(jnp.bfloat16)
    spatial = lax.all_to_all(along_rows, "lon", split_axis=2, concat_axis=1, tiled=True)
    mixed = jnp.einsum(
        "cd,cp->dp", mix_weight, spatial.reshape(channels, -1), preferred_element_type=jnp.float32
    )
    wet_flat = wet_grid.reshape(1, -1).astype(jnp.float32)
    output = wet_flat * (residual.reshape(channels, -1).astype(jnp.float32) + mixed)
    return output.astype(jnp.bfloat16).reshape(field.shape)


def solution(mesh):
    placed = (P(None, "lat", "lon"), P("lat", "lon"), P(), P(), P(), P(), P(), P(), P())
    return jax.shard_map(
        local, mesh=mesh, in_specs=placed, out_specs=P(None, "lat", "lon"), check_vma=False
    )
```

profile of v0, /device:TPU:24, one launch (start us, length us, event | category | flops | bytes accessed | tf_op | source)
XLA Modules:
  0.0 204.7 jit_solution(11672251696216430919)
XLA Ops:
  0.9 4.5 %copy.33 = bf16[150,16,256]{0,1,2:T(8,128)(2,1)} copy(bf16[150,16,256]{2,1,0:T(8,128)(2,1)} %param.11) | data formatting | bytes 2457600 | tf_op args[0]
  5.4 1.9 broadcast_multiply_fusion.1
  8.0 1.7 collective-permute-start.1
  12.7 9.4 %all_gather.3 = bf16[150,3,1024]{2,0,1:T(8,128)(2,1)S(1)} all-gather(bf16[150,3,256]{2,0,1:T(8,128)(2,1)S(1)} %copy.36), channel_id=1, replica_groups=mesh['lat'=8,'lon'=4] {'lon'}, dimensions={2}, use_global_device_ids=true | all-gather | bytes 1152000 | tf_op jit(solution)/shard_map/all_gather | solution.py:81
  22.2 1.7 gather_fusion
  27.3 3.3 %collective-permute-start.3 = (bf16[150,3,262]{2,0,1:T(8,128)(2,1)S(1)}, bf16[150,3,262]{2,0,1:T(8,128)(2,1)}, u32[]{:S(2)}, u32[]{:S(2)}) collective-permute-start(bf16[150,3,262]{2,0,1:T(8,128)(2,1)S(1)} %copy.38), channel_id=1, source_target_pairs={{4,0},{8,4},{12,8},{16,12},{20,16},{24,20},{28,24},{5,1},{9,5},{13... | collective-permute-start | bytes 707408 | tf_op jit(solution)/shard_map/ppermute | solution.py:18
  30.7 3.2 %copy.40 = bf16[150,16,256]{2,1,0:T(8,128)(2,1)} copy(bf16[150,16,256]{0,1,2:T(8,128)(2,1)S(1)} %broadcast_multiply_fusion.1) | data formatting | bytes 2457600 | tf_op jit(solution)/shard_map/while | solution.py:106
  33.9 2.5 %copy.37 = bf16[150,3,1024]{0,1,2:T(4,128)(2,1)} copy(bf16[150,3,1024]{2,0,1:T(8,128)(2,1)S(1)} %all_gather.3) | data formatting | bytes 1843200 | tf_op jit(solution)/shard_map/all_gather | solution.py:81
  36.4 3.6 %gather_fusion.1 = bf16[262,150,3]{1,2,0:T(4,128)(2,1)} fusion(bf16[150,3,1024]{0,1,2:T(4,128)(2,1)} %copy.37, s32[1024]{0:T(1024)S(1)} %pad_clamp_fusion), kind=kCustom, calls=%fused_computation.1 | custom fusion | bytes 472648 | tf_op jit(solution)/shard_map/jit(_take)/gather | solution.py:84
  40.0 1.6 fusion.48
  41.6 2.1 %copy.34 = bf16[150,3,262]{2,0,1:T(8,128)(2,1)} copy(bf16[150,3,262]{0,1,2:T(4,128)(2,1)} %get-tuple-element.195) | data formatting | bytes 471600 | tf_op jit(solution)/shard_map/slice | solution.py:13
  43.7 3.4 %collective-permute-start.2 = (bf16[150,3,262]{2,0,1:T(8,128)(2,1)}, bf16[150,3,262]{2,0,1:T(8,128)(2,1)}, u32[]{:S(2)}, u32[]{:S(2)}) collective-permute-start(bf16[150,3,262]{2,0,1:T(8,128)(2,1)} %copy.34), channel_id=1, source_target_pairs={{0,4},{4,8},{8,12},{12,16},{16,20},{20,24},{24,28},{1,5},{5,9},{9,... | collective-permute-start | bytes 707408 | tf_op jit(solution)/shard_map/ppermute | solution.py:16
  48.5 2.0 bitcast_select_fusion
  50.5 6.5 %collective-permute-done.2 = bf16[150,3,262]{2,0,1:T(8,128)(2,1)} collective-permute-done((bf16[150,3,262]{2,0,1:T(8,128)(2,1)}, bf16[150,3,262]{2,0,1:T(8,128)(2,1)}, u32[]{:S(2)}, u32[]{:S(2)}) %collective-permute-start.2) | collective-permute-done | bytes 235832 | tf_op jit(solution)/shard_map/ppermute | solution.py:16
  58.7 5.1 %maximum_maximum_fusion = (bf16[150,19,262]{0,1,2:T(8,128)(2,1)S(1)}, bf16[150,19,262]{0,1,2:T(8,128)(2,1)S(1)}) fusion(bf16[150,16,3]{0,1,2:T(8,128)(2,1)S(1)} %collective-permute-done.1, bf16[150,16,256]{0,1,2:T(8,128)(2,1)S(1)} %broadcast_multiply_fusion.1, bf16[150,16,3]{0,1,2:T(8,128)(2,1)S(1)} %collective-permute-done, ...), kind=kLoop, calls=%fused_computation.36 | loop fusion | flops 11947200 | bytes 4716000 | tf_op jit(solution)/shard_map/concatenate | solution.py:90
  64.2 41.2 %multiply_add_fusion = f32[150,16,256]{0,1,2:T(8,128)} fusion(bf16[150,16,256]{0,1,2:T(8,128)(2,1)S(1)} %broadcast_multiply_fusion.1, bf16[150,16,3]{0,1,2:T(8,128)(2,1)S(1)} %collective-permute-done.1, bf16[150,16,3]{0,1,2:T(8,128)(2,1)S(1)} %collective-permute-done, bf16[150,19,262]{0,1,2:T(8,128)(2,1)S(1)} %get-tuple-element.194, ...), kind=kLoop, calls=%fused_computation.35 | loop fusion | flops 93388800 | bytes 55354200 | tf_op jit(solution)/shard_map/add | solution.py:51
  105.5 5.2 %copy.41 = f32[150,16,256]{2,1,0:T(8,128)} copy(f32[150,16,256]{0,1,2:T(8,128)} %multiply_add_fusion) | data formatting | bytes 4915200 | tf_op jit(solution)/shard_map/while | solution.py:106
  111.7 16.3 %while.13 = (s32[]{:T(128)}, bf16[150,16,256]{2,1,0:T(8,128)(2,1)}, bf16[16,256]{1,0:T(8,128)(2,1)S(1)}, bf16[150,16,256]{2,1,0:T(8,128)(2,1)}, f32[150,16,256]{...) while((s32[]{:T(128)}, bf16[150,16,256]{2,1,0:T(8,128)(2,1)}, ...), condition=%wide.region_3.4_spmd, body=%wide.region_0.3_spmd.sunk | while | flops 752029696 | bytes 21516636 | solution.py:106
  115.7 3.1 %fusion.65 = bf16[150,2048]{1,0:T(8,128)(2,1)S(1)} fusion(f32[150,2048]{1,0:T(8,128)S(1)} %bitcast.157, bf16[600,150]{0,1:T(8,128)(2,1)} %get-tuple-element.344, bf16[150,600]{1,0:T(8,128)(2,1)S(1)} %get-tuple-element.343, f32[150,2048]{1,0:T(8,128)S(1)} %bitcast.156, f32[150]{0:T(256)S(1)} %get-tuple-element.342, f32[2048]{0:T(1024)S(1)} %bitcast.165, ...), kind=kOutput, calls=%fused_computation.14.clone.1 | convolution fusion | flops 750489600 | bytes 3457176 | tf_op jit(solution)/shard_map/while/body/eval_jaxpr/hc,hp->cp/dot_general | solution.py:66
  123.9 3.1 %fusion.65 = bf16[150,2048]{1,0:T(8,128)(2,1)S(1)} fusion(f32[150,2048]{1,0:T(8,128)S(1)} %bitcast.157, bf16[600,150]{0,1:T(8,128)(2,1)} %get-tuple-element.344, bf16[150,600]{1,0:T(8,128)(2,1)S(1)} %get-tuple-element.343, f32[150,2048]{1,0:T(8,128)S(1)} %bitcast.156, f32[150]{0:T(256)S(1)} %get-tuple-element.342, f32[2048]{0:T(1024)S(1)} %bitcast.165, ...), kind=kOutput, calls=%fused_computation.14.clone.1 | convolution fusion | flops 750489600 | bytes 3457176 | tf_op jit(solution)/shard_map/while/body/eval_jaxpr/hc,hp->cp/dot_general | solution.py:66
  128.1 2.8 %copy.43 = bf16[150,16,256]{2,0,1:T(8,128)(2,1)} copy(bf16[150,16,256]{2,1,0:T(8,128)(2,1)} %get-tuple-element.144) | data formatting | bytes 2457600 | tf_op jit(solution)/shard_map/while | solution.py:106
  130.9 3.8 %all-to-all-start = ((bf16[150,16,256]{2,0,1:T(8,128)(2,1)}), bf16[150,16,256]{2,0,1:T(8,128)(2,1)S(1)}, u32[]{:S(2)}, u32[]{:S(2)}) async-start(bf16[150,16,256]{2,0,1:T(8,128)(2,1)} %copy.43), calls=%async_computation | async-start | bytes 2490368 | tf_op jit(solution)/shard_map/all_to_all | solution.py:109
  135.2 9.3 %multiply_convert_fusion.3 = (bf16[1024,512]{1,0:T(8,128)(2,1)}, bf16[1024,512]{1,0:T(8,128)(2,1)}) fusion(), kind=kLoop, calls=%fused_computation.55 | loop fusion | flops 9961472 | bytes 2097152 | tf_op jit(solution)/shard_map/convert.7
  144.6 6.4 %all-to-all-done = bf16[150,16,256]{2,0,1:T(8,128)(2,1)S(1)} async-done(((bf16[150,16,256]{2,0,1:T(8,128)(2,1)}), bf16[150,16,256]{2,0,1:T(8,128)(2,1)S(1)}, u32[]{:S(2)}, u32[]{:S(2)}) %all-to-all-start) | async-done | bytes 1228832 | tf_op jit(solution)/shard_map/all_to_all | solution.py:109
  152.7 3.0 %fusion.35 = f32[150,4,1024]{2,0,1:T(8,128)S(1)} fusion(bf16[150,4,1024]{2,0,1:T(8,128)(2,1)S(1)} %dot_general.27, bf16[1024,512]{1,0:T(8,128)(2,1)} %get-tuple-element.250, bf16[1024,512]{1,0:T(8,128)(2,1)} %get-tuple-element.251), kind=kOutput, calls=%fused_computation.61 | convolution fusion | flops 1262485504 | bytes 5783552 | tf_op jit(solution)/shard_map/dot_general | solution.py:112
  158.8 2.5 %copy.46 = bf16[150,4,1024]{0,1,2:T(4,128)(2,1)} copy(bf16[150,4,1024]{2,0,1:T(8,128)(2,1)S(1)} %convolution_convert_fusion) | data formatting | bytes 2457600 | tf_op jit(solution)/shard_map/convert_element_type | solution.py:122
  161.3 4.5 %all-to-all-start.1 = ((bf16[150,4,1024]{0,1,2:T(4,128)(2,1)}), bf16[150,4,1024]{0,1,2:T(4,128)(2,1)}, u32[]{:S(2)}, u32[]{:S(2)}) async-start(bf16[150,4,1024]{0,1,2:T(4,128)(2,1)} %copy.46), calls=%async_computation.1 | async-start | bytes 4194304 | tf_op jit(solution)/shard_map/all_to_all | solution.py:123
  166.1 2.0 copy.60
  168.2 23.3 %all-to-all-done.1 = bf16[150,4,1024]{0,1,2:T(4,128)(2,1)} async-done(((bf16[150,4,1024]{0,1,2:T(4,128)(2,1)}), bf16[150,4,1024]{0,1,2:T(4,128)(2,1)}, u32[]{:S(2)}, u32[]{:S(2)}) %all-to-all-start.1) | async-done | bytes 1228832 | tf_op jit(solution)/shard_map/all_to_all | solution.py:123
  191.5 6.3 %copy.48 = bf16[150,4,4,256]{3,2,1,0:T(4,128)(2,1)} copy(bf16[150,4,4,256]{0,2,3,1:T(4,128)(2,1)} %bitcast.59) | data formatting | bytes 2457600 | tf_op jit(solution)/shard_map/all_to_all | solution.py:123
  197.8 3.5 %reshape.188 = bf16[150,4096]{1,0:T(8,128)(2,1)} reshape(bf16[150,4,4,256]{3,2,1,0:T(4,128)(2,1)} %copy.48) | data formatting | bytes 2457600 | tf_op jit(solution)/shard_map/reshape | solution.py:125
  201.3 1.9 fusion.24
  (160 shorter events, 28.9 us)
Async XLA Ops:
  0.0 201.3 %copy-start = (bf16[150,150]{1,0:T(8,128)(2,1)S(1)}, bf16[150,150]{1,0:T(8,128)(2,1)}, u32[]{:S(2)}) copy-start(bf16[150,150]{1,0:T(8,128)(2,1)} %param.19) | copy-start | bytes 135004
  0.9 9.1 %copy-start.6 = (f32[150,7,7]{0,2,1:T(8,128)S(1)}, f32[150,7,7]{0,2,1:T(8,128)}, u32[]{:S(2)}) copy-start(f32[150,7,7]{0,2,1:T(8,128)} %param.14) | copy-start | bytes 88204
  5.4 16.8 %copy-start.1 = (s32[1024]{0:T(1024)S(1)}, s32[1024]{0:T(1024)}, u32[]{:S(2)}) copy-start(s32[1024]{0:T(1024)} %param.13) | copy-start | bytes 12292
  8.0 16.5 %collective-permute-start = (bf16[150,16,3]{0,1,2:T(8,128)(2,1)}, bf16[150,16,3]{0,1,2:T(8,128)(2,1)S(1)}, u32[]{:S(2)}, u32[]{:S(2)}) collective-permute-start(bf16[150,16,3]{0,1,2:T(8,128)(2,1)} %get-tuple-element.197), channel_id=1, source_target_pairs={{0,1},{1,2},{2,3},{3,0},{4,5},{5,6},{6,7},{7,4},{8,9},{9,10},{10,1... | collective-permute-start | bytes 43208 | tf_op jit(solution)/shard_map/ppermute | solution.py:16
  8.0 16.5 %collective-permute-start.1 = (bf16[150,16,3]{0,1,2:T(8,128)(2,1)}, bf16[150,16,3]{0,1,2:T(8,128)(2,1)S(1)}, u32[]{:S(2)}, u32[]{:S(2)}) collective-permute-start(bf16[150,16,3]{0,1,2:T(8,128)(2,1)} %get-tuple-element.198), channel_id=1, source_target_pairs={{1,0},{2,1},{3,2},{0,3},{5,4},{6,5},{7,6},{4,7},{9,8},{10,9},{11,1... | collective-permute-start | bytes 43208 | tf_op jit(solution)/shard_map/ppermute | solution.py:18
  27.3 19.8 %collective-permute-start.3 = (bf16[150,3,262]{2,0,1:T(8,128)(2,1)S(1)}, bf16[150,3,262]{2,0,1:T(8,128)(2,1)}, u32[]{:S(2)}, u32[]{:S(2)}) collective-permute-start(bf16[150,3,262]{2,0,1:T(8,128)(2,1)S(1)} %copy.38), channel_id=1, source_target_pairs={{4,0},{8,4},{12,8},{16,12},{20,16},{24,20},{28,24},{5,1},{9,5},{13... | collective-permute-start | bytes 707408 | tf_op jit(solution)/shard_map/ppermute | solution.py:18
  30.7 17.8 %copy-start.46 = (pred[262]{0:T(512)(128)(4,1)S(1)}, pred[262]{0:T(512)(128)(4,1)}, u32[]{:S(2)}) copy-start(pred[262]{0:T(512)(128)(4,1)} %compare_and_fusion) | copy-start | bytes 790
  43.7 13.3 %collective-permute-start.2 = (bf16[150,3,262]{2,0,1:T(8,128)(2,1)}, bf16[150,3,262]{2,0,1:T(8,128)(2,1)}, u32[]{:S(2)}, u32[]{:S(2)}) collective-permute-start(bf16[150,3,262]{2,0,1:T(8,128)(2,1)} %copy.34), channel_id=1, source_target_pairs={{0,4},{4,8},{8,12},{12,16},{16,20},{20,24},{24,28},{1,5},{5,9},{9,... | collective-permute-start | bytes 707408 | tf_op jit(solution)/shard_map/ppermute | solution.py:16
  58.3 5.5 %copy-start.7 = (f32[150,1,1]{0,2,1:T(1,128)S(1)}, f32[150,1,1]{0,2,1:T(1,128)}, u32[]{:S(2)}) copy-start(f32[150,1,1]{0,2,1:T(1,128)} %get-tuple-element.223) | copy-start | bytes 1804
  58.3 5.5 %copy-start.8 = (f32[150,1,1]{0,2,1:T(1,128)S(1)}, f32[150,1,1]{0,2,1:T(1,128)}, u32[]{:S(2)}) copy-start(f32[150,1,1]{0,2,1:T(1,128)} %get-tuple-element.224) | copy-start | bytes 1804
  58.4 5.5 %copy-start.9 = (f32[150,1,1]{0,2,1:T(1,128)S(1)}, f32[150,1,1]{0,2,1:T(1,128)}, u32[]{:S(2)}) copy-start(f32[150,1,1]{0,2,1:T(1,128)} %get-tuple-element.225) | copy-start | bytes 1804
  58.4 5.5 %copy-start.10 = (f32[150,1,1]{0,2,1:T(1,128)S(1)}, f32[150,1,1]{0,2,1:T(1,128)}, u32[]{:S(2)}) copy-start(f32[150,1,1]{0,2,1:T(1,128)} %get-tuple-element.226) | copy-start | bytes 1804
  58.4 5.5 %copy-start.11 = (f32[150,1,1]{0,2,1:T(1,128)S(1)}, f32[150,1,1]{0,2,1:T(1,128)}, u32[]{:S(2)}) copy-start(f32[150,1,1]{0,2,1:T(1,128)} %get-tuple-element.227) | copy-start | bytes 1804
  58.4 5.5 %copy-start.12 = (f32[150,1,1]{0,2,1:T(1,128)S(1)}, f32[150,1,1]{0,2,1:T(1,128)}, u32[]{:S(2)}) copy-start(f32[150,1,1]{0,2,1:T(1,128)} %get-tuple-element.228) | copy-start | bytes 1804
  58.4 5.5 %copy-start.13 = (f32[150,1,1]{0,2,1:T(1,128)S(1)}, f32[150,1,1]{0,2,1:T(1,128)}, u32[]{:S(2)}) copy-start(f32[150,1,1]{0,2,1:T(1,128)} %get-tuple-element.229) | copy-start | bytes 1804
  58.4 5.5 %copy-start.14 = (f32[150,1,1]{0,2,1:T(1,128)S(1)}, f32[150,1,1]{0,2,1:T(1,128)}, u32[]{:S(2)}) copy-start(f32[150,1,1]{0,2,1:T(1,128)} %get-tuple-element.230) | copy-start | bytes 1804
  58.4 5.5 %copy-start.15 = (f32[150,1,1]{0,2,1:T(1,128)S(1)}, f32[150,1,1]{0,2,1:T(1,128)}, u32[]{:S(2)}) copy-start(f32[150,1,1]{0,2,1:T(1,128)} %get-tuple-element.231) | copy-start | bytes 1804
  58.4 5.5 %copy-start.16 = (f32[150,1,1]{0,2,1:T(1,128)S(1)}, f32[150,1,1]{0,2,1:T(1,128)}, u32[]{:S(2)}) copy-start(f32[150,1,1]{0,2,1:T(1,128)} %get-tuple-element.232) | copy-start | bytes 1804
  58.4 5.5 %copy-start.17 = (f32[150,1,1]{0,2,1:T(1,128)S(1)}, f32[150,1,1]{0,2,1:T(1,128)}, u32[]{:S(2)}) copy-start(f32[150,1,1]{0,2,1:T(1,128)} %get-tuple-element.233) | copy-start | bytes 1804
  58.4 5.5 %copy-start.18 = (f32[150,1,1]{0,2,1:T(1,128)S(1)}, f32[150,1,1]{0,2,1:T(1,128)}, u32[]{:S(2)}) copy-start(f32[150,1,1]{0,2,1:T(1,128)} %get-tuple-element.234) | copy-start | bytes 1804
  58.5 5.5 %copy-start.19 = (f32[150,1,1]{0,2,1:T(1,128)S(1)}, f32[150,1,1]{0,2,1:T(1,128)}, u32[]{:S(2)}) copy-start(f32[150,1,1]{0,2,1:T(1,128)} %get-tuple-element.235) | copy-start | bytes 1804
  58.5 5.5 %copy-start.20 = (f32[150,1,1]{0,2,1:T(1,128)S(1)}, f32[150,1,1]{0,2,1:T(1,128)}, u32[]{:S(2)}) copy-start(f32[150,1,1]{0,2,1:T(1,128)} %get-tuple-element.236) | copy-start | bytes 1804
  58.5 5.5 %copy-start.21 = (f32[150,1,1]{0,2,1:T(1,128)S(1)}, f32[150,1,1]{0,2,1:T(1,128)}, u32[]{:S(2)}) copy-start(f32[150,1,1]{0,2,1:T(1,128)} %get-tuple-element.237) | copy-start | bytes 1804
  58.5 5.5 %copy-start.22 = (f32[150,1,1]{0,2,1:T(1,128)S(1)}, f32[150,1,1]{0,2,1:T(1,128)}, u32[]{:S(2)}) copy-start(f32[150,1,1]{0,2,1:T(1,128)} %get-tuple-element.238) | copy-start | bytes 1804
  58.5 5.5 %copy-start.23 = (f32[150,1,1]{0,2,1:T(1,128)S(1)}, f32[150,1,1]{0,2,1:T(1,128)}, u32[]{:S(2)}) copy-start(f32[150,1,1]{0,2,1:T(1,128)} %get-tuple-element.239) | copy-start | bytes 1804
  58.5 5.5 %copy-start.24 = (f32[150,1,1]{0,2,1:T(1,128)S(1)}, f32[150,1,1]{0,2,1:T(1,128)}, u32[]{:S(2)}) copy-start(f32[150,1,1]{0,2,1:T(1,128)} %get-tuple-element.240) | copy-start | bytes 1804
  105.5 6.3 %copy-start.47 = (bf16[150,600]{1,0:T(8,128)(2,1)S(1)}, bf16[150,600]{1,0:T(8,128)(2,1)}, u32[]{:S(2)}) copy-start(bf16[150,600]{1,0:T(8,128)(2,1)} %param.16) | copy-start | bytes 540004
  105.5 6.3 %copy-start.48 = (f32[150]{0:T(256)S(1)}, f32[150]{0:T(256)}, u32[]{:S(2)}) copy-start(f32[150]{0:T(256)} %param.15) | copy-start | bytes 1804
  128.1 6.6 %copy-start.5 = (f32[2,150,512]{2,0,1:T(2,128)S(1)}, f32[2,150,512]{2,0,1:T(2,128)}, u32[]{:S(2)}) copy-start(f32[2,150,512]{2,0,1:T(2,128)} %param.18) | copy-start | bytes 1843204
  130.9 20.0 %all-to-all-start = ((bf16[150,16,256]{2,0,1:T(8,128)(2,1)}), bf16[150,16,256]{2,0,1:T(8,128)(2,1)S(1)}, u32[]{:S(2)}, u32[]{:S(2)}) async-start(bf16[150,16,256]{2,0,1:T(8,128)(2,1)} %copy.43), calls=%async_computation | async-start | bytes 2490368 | tf_op jit(solution)/shard_map/all_to_all | solution.py:109
  158.7 7.0 %copy-start.2 = (bf16[150,16,256]{2,1,0:T(8,128)(2,1)S(1)}, bf16[150,16,256]{2,1,0:T(8,128)(2,1)}, u32[]{:S(2)}) copy-start(bf16[150,16,256]{2,1,0:T(8,128)(2,1)} %get-tuple-element.144) | copy-start | bytes 3686404
  161.3 30.2 %all-to-all-start.1 = ((bf16[150,4,1024]{0,1,2:T(4,128)(2,1)}), bf16[150,4,1024]{0,1,2:T(4,128)(2,1)}, u32[]{:S(2)}, u32[]{:S(2)}) async-start(bf16[150,4,1024]{0,1,2:T(4,128)(2,1)} %copy.46), calls=%async_computation.1 | async-start | bytes 4194304 | tf_op jit(solution)/shard_map/all_to_all | solution.py:123
  (23 other events, 118.4 us)
where the time goes:
time: 206 us; the launch traced here: 205 us
  other arithmetic  68.6 us (33%)
  local copies, waits for them, and re-layouts  60 us (29%)
  waiting for transfers between devices  36.2 us (18%)
  starting transfers between devices  16.7 us (8%)
  matrix products  12.6 us (6%)
  blocking collectives  9.4 us (5%)
    add x1, other arithmetic, depthwise_conv(): total + weight_col * extended[:, tap_row:tap_row + lat_rows, tap_col:tap_...  41.2 us
    all_to_all x1, waiting for transfers between devices, local(): lax.all_to_all(along_rows, 'lon', split_axis=2, concat_axis=1, tiled=True)  23.3 us
    while x3, local copies, waits for them, and re-layouts, local(): lax.fori_loop(0, lat_rows // group_rows, mix_rows, jnp.zeros(field.shape,...  11.2 us
    another operation x2, other arithmetic  9.82 us
    all_gather x1, blocking collectives, local(): fold_full = lax.all_gather(top_rows, 'lon', axis=2, tiled=True)  9.4 us
    unnamed x103, local copies, waits for them, and re-layouts  8.46 us
    ppermute x2, waiting for transfers between devices, extended_2(): lax.ppermute(tail, axis, [(i, (i + 1) % count) for i in range(ends)])  6.5 us
    all_to_all x1, waiting for transfers between devices, local(): lax.all_to_all(residual, 'lon', split_axis=1, concat_axis=2, tiled=True)  6.4 us
  transfers between devices with their start and end apart: 6, of which 3 were waited for; matrix products, arithmetic and copies ran while one was open for 17% of the time, Pallas kernels for 0%

commit v1 on v0

--- a/solution.py
+++ b/solution.py
@@ -120,7 +120,10 @@
     along_rows = jnp.einsum(
         "crk,nk->crn", scaled, fourier, preferred_element_type=jnp.float32
     ).astype(jnp.bfloat16)
-    spatial = lax.all_to_all(along_rows, "lon", split_axis=2, concat_axis=1, tiled=True)
+    spatial = jnp.concatenate(
+        lax.all_to_all(jnp.stack(jnp.split(along_rows, lax.axis_size("lon"), axis=2)), "lon", 0, 0),
+        axis=1,
+    )
     mixed = jnp.einsum(
         "cd,cp->dp", mix_weight, spatial.reshape(channels, -1), preferred_element_type=jnp.float32
     )

time: 206 us -> 192 us (0.932)
  waiting for transfers between devices: 36.2 us -> 26.9 us
  local copies, waits for them, and re-layouts: 60 us -> 55.5 us
    all_to_all x1, waiting for transfers between devices: 23.3 us -> 14 us  [local(): lax.all_to_all(jnp.stack(jnp.split(along_rows, lax.axis_size('lon'), axis...]
    all_to_all x1 -> x0, local copies, waits for them, and re-layouts: 6.32 us -> none  [local(): lax.all_to_all(along_rows, 'lon', split_axis=2, concat_axis=1, tiled=True)]
    another operation x0 -> x3, local copies, waits for them, and re-layouts: none -> 5.14 us  [the longest x1 3.56 us: local(): spatial.reshape(channels, -1)]
    convert_element_type x1 -> x0, local copies, waits for them, and re-layouts: 2.54 us -> none  [local(): along_rows = jnp.einsum('crk,nk->crn', scaled, fourier, preferred_element...]
    another operation x2 -> x3, other arithmetic: 9.82 us -> 9.98 us
  transfers between devices with their start and end apart: 6 -> 6, of which waited for: 3 -> 3; matrix products, arithmetic and copies ran while one was open for 17% -> 18% of each run, Pallas kernels for 0% -> 0%
where the time goes in v1:
time: 192 us; the launch traced here: 191 us
  other arithmetic  68.9 us (36%)
  local copies, waits for them, and re-layouts  55.5 us (29%)
  waiting for transfers between devices  26.9 us (14%)
  starting transfers between devices  16.5 us (9%)
  matrix products  12.6 us (7%)
  blocking collectives  9.4 us (5%)
    add x1, other arithmetic, depthwise_conv(): total + weight_col * extended[:, tap_row:tap_row + lat_rows, tap_col:tap_...  41.2 us
    all_to_all x1, waiting for transfers between devices, local(): lax.all_to_all(jnp.stack(jnp.split(along_rows, lax.axis_size('lon'), axis...  14 us
    while x3, local copies, waits for them, and re-layouts, local(): lax.fori_loop(0, lat_rows // group_rows, mix_rows, jnp.zeros(field.shape,...  11.2 us
    another operation x2, other arithmetic  9.82 us
    all_gather x1, blocking collectives, local(): fold_full = lax.all_gather(top_rows, 'lon', axis=2, tiled=True)  9.4 us
    unnamed x103, local copies, waits for them, and re-layouts  8.46 us
    ppermute x2, waiting for transfers between devices, extended_2(): lax.ppermute(tail, axis, [(i, (i + 1) % count) for i in range(ends)])  6.49 us
    all_to_all x1, waiting for transfers between devices, local(): lax.all_to_all(residual, 'lon', split_axis=1, concat_axis=2, tiled=True)  6.4 us
  transfers between devices with their start and end apart: 6, of which 3 were waited for; matrix products, arithmetic and copies ran while one was open for 18% of the time, Pallas kernels for 0%

profile of v1, /device:TPU:24, one launch (start us, length us, event | category | flops | bytes accessed | tf_op | source)
XLA Modules:
  0.0 190.9 jit_solution(7563220064580239137)
XLA Ops:
  0.9 4.5 %copy.32 = bf16[150,16,256]{0,1,2:T(8,128)(2,1)} copy(bf16[150,16,256]{2,1,0:T(8,128)(2,1)} %param.11) | data formatting | bytes 2457600 | tf_op args[0]
  5.4 1.9 %broadcast_multiply_fusion.1 = bf16[150,16,256]{0,1,2:T(8,128)(2,1)S(1)} fusion(bf16[150,16,256]{0,1,2:T(8,128)(2,1)} %copy.32, bf16[16,256]{0,1:T(8,128)(2,1)S(1)} %copy.31), kind=kLoop, calls=%fused_computation.69 | loop fusion | flops 614400 | bytes 2465792 | tf_op jit(solution)/shard_map/mul | solution.py:79
  8.0 1.7 collective-permute-start.1
  12.8 9.4 %all_gather.3 = bf16[150,3,1024]{2,0,1:T(8,128)(2,1)S(1)} all-gather(bf16[150,3,256]{2,0,1:T(8,128)(2,1)S(1)} %copy.35), channel_id=1, replica_groups=mesh['lat'=8,'lon'=4] {'lon'}, dimensions={2}, use_global_device_ids=true | all-gather | bytes 1152000 | tf_op jit(solution)/shard_map/all_gather | solution.py:81
  22.2 1.7 gather_fusion
  27.4 3.3 %collective-permute-start.3 = (bf16[150,3,262]{2,0,1:T(8,128)(2,1)S(1)}, bf16[150,3,262]{2,0,1:T(8,128)(2,1)}, u32[]{:S(2)}, u32[]{:S(2)}) collective-permute-start(bf16[150,3,262]{2,0,1:T(8,128)(2,1)S(1)} %copy.37), channel_id=1, source_target_pairs={{4,0},{8,4},{12,8},{16,12},{20,16},{24,20},{28,24},{5,1},{9,5},{13... | collective-permute-start | bytes 707408 | tf_op jit(solution)/shard_map/ppermute | solution.py:18
  30.7 3.2 %copy.39 = bf16[150,16,256]{2,1,0:T(8,128)(2,1)} copy(bf16[150,16,256]{0,1,2:T(8,128)(2,1)S(1)} %broadcast_multiply_fusion.1) | data formatting | bytes 2457600 | tf_op jit(solution)/shard_map/while | solution.py:106
  33.9 2.5 %copy.36 = bf16[150,3,1024]{0,1,2:T(4,128)(2,1)} copy(bf16[150,3,1024]{2,0,1:T(8,128)(2,1)S(1)} %all_gather.3) | data formatting | bytes 1843200 | tf_op jit(solution)/shard_map/all_gather | solution.py:81
  36.4 3.6 %gather_fusion.1 = bf16[262,150,3]{1,2,0:T(4,128)(2,1)} fusion(bf16[150,3,1024]{0,1,2:T(4,128)(2,1)} %copy.36, s32[1024]{0:T(1024)S(1)} %pad_clamp_fusion), kind=kCustom, calls=%fused_computation.1 | custom fusion | bytes 472648 | tf_op jit(solution)/shard_map/jit(_take)/gather | solution.py:84
  40.1 1.6 fusion.48
  41.7 2.1 %copy.33 = bf16[150,3,262]{2,0,1:T(8,128)(2,1)} copy(bf16[150,3,262]{0,1,2:T(4,128)(2,1)} %get-tuple-element.195) | data formatting | bytes 471600 | tf_op jit(solution)/shard_map/slice | solution.py:13
  43.8 3.4 %collective-permute-start.2 = (bf16[150,3,262]{2,0,1:T(8,128)(2,1)}, bf16[150,3,262]{2,0,1:T(8,128)(2,1)}, u32[]{:S(2)}, u32[]{:S(2)}) collective-permute-start(bf16[150,3,262]{2,0,1:T(8,128)(2,1)} %copy.33), channel_id=1, source_target_pairs={{0,4},{4,8},{8,12},{12,16},{16,20},{20,24},{24,28},{1,5},{5,9},{9,... | collective-permute-start | bytes 707408 | tf_op jit(solution)/shard_map/ppermute | solution.py:16
  48.6 2.0 %bitcast_select_fusion = bf16[150,3,262]{0,1,2:T(4,128)(2,1)S(1)} fusion(bf16[150,3,262]{0,1,2:T(4,128)(2,1)S(1)} %copy.38, bf16[262,150,3]{1,2,0:T(4,128)(2,1)} %gather_fusion.1, pred[262]{0:T(512)(128)(4,1)S(1)} %copy-done.46, pred[]{:T(512)S(6)} %eq.7), kind=kLoop, calls=%fused_computation.73 | loop fusion | flops 235800 | bytes 707663 | tf_op jit(solution)/shard_map/jit(_where)/select_n | solution.py:89
  50.6 6.5 %collective-permute-done.2 = bf16[150,3,262]{2,0,1:T(8,128)(2,1)} collective-permute-done((bf16[150,3,262]{2,0,1:T(8,128)(2,1)}, bf16[150,3,262]{2,0,1:T(8,128)(2,1)}, u32[]{:S(2)}, u32[]{:S(2)}) %collective-permute-start.2) | collective-permute-done | bytes 235832 | tf_op jit(solution)/shard_map/ppermute | solution.py:16
  58.8 5.1 %maximum_maximum_fusion = (bf16[150,19,262]{0,1,2:T(8,128)(2,1)S(1)}, bf16[150,19,262]{0,1,2:T(8,128)(2,1)S(1)}) fusion(bf16[150,16,3]{0,1,2:T(8,128)(2,1)S(1)} %collective-permute-done.1, bf16[150,16,256]{0,1,2:T(8,128)(2,1)S(1)} %broadcast_multiply_fusion.1, bf16[150,16,3]{0,1,2:T(8,128)(2,1)S(1)} %collective-permute-done, ...), kind=kLoop, calls=%fused_computation.36 | loop fusion | flops 11947200 | bytes 4716000 | tf_op jit(solution)/shard_map/concatenate | solution.py:90
  64.3 41.2 %multiply_add_fusion = f32[150,16,256]{0,1,2:T(8,128)} fusion(bf16[150,16,256]{0,1,2:T(8,128)(2,1)S(1)} %broadcast_multiply_fusion.1, bf16[150,16,3]{0,1,2:T(8,128)(2,1)S(1)} %collective-permute-done.1, bf16[150,16,3]{0,1,2:T(8,128)(2,1)S(1)} %collective-permute-done, bf16[150,19,262]{0,1,2:T(8,128)(2,1)S(1)} %get-tuple-element.194, ...), kind=kLoop, calls=%fused_computation.35 | loop fusion | flops 93388800 | bytes 55354200 | tf_op jit(solution)/shard_map/add | solution.py:51
  105.6 5.1 %copy.40 = f32[150,16,256]{2,1,0:T(8,128)} copy(f32[150,16,256]{0,1,2:T(8,128)} %multiply_add_fusion) | data formatting | bytes 4915200 | tf_op jit(solution)/shard_map/while | solution.py:106
  111.8 16.3 %while.13 = (s32[]{:T(128)}, bf16[150,16,256]{2,1,0:T(8,128)(2,1)}, bf16[16,256]{1,0:T(8,128)(2,1)S(1)}, bf16[150,16,256]{2,1,0:T(8,128)(2,1)}, f32[150,16,256]{...) while((s32[]{:T(128)}, bf16[150,16,256]{2,1,0:T(8,128)(2,1)}, ...), condition=%wide.region_3.4_spmd, body=%wide.region_0.3_spmd.sunk | while | flops 752029696 | bytes 21516636 | solution.py:106
  115.8 3.1 %fusion.65 = bf16[150,2048]{1,0:T(8,128)(2,1)S(1)} fusion(f32[150,2048]{1,0:T(8,128)S(1)} %bitcast.162, bf16[600,150]{0,1:T(8,128)(2,1)} %get-tuple-element.348, bf16[150,600]{1,0:T(8,128)(2,1)S(1)} %get-tuple-element.347, f32[150,2048]{1,0:T(8,128)S(1)} %bitcast.161, f32[150]{0:T(256)S(1)} %get-tuple-element.346, f32[2048]{0:T(1024)S(1)} %bitcast.170, ...), kind=kOutput, calls=%fused_computation.14.clone.1 | convolution fusion | flops 750489600 | bytes 3457176 | tf_op jit(solution)/shard_map/while/body/eval_jaxpr/hc,hp->cp/dot_general | solution.py:66
  124.0 3.1 %fusion.65 = bf16[150,2048]{1,0:T(8,128)(2,1)S(1)} fusion(f32[150,2048]{1,0:T(8,128)S(1)} %bitcast.162, bf16[600,150]{0,1:T(8,128)(2,1)} %get-tuple-element.348, bf16[150,600]{1,0:T(8,128)(2,1)S(1)} %get-tuple-element.347, f32[150,2048]{1,0:T(8,128)S(1)} %bitcast.161, f32[150]{0:T(256)S(1)} %get-tuple-element.346, f32[2048]{0:T(1024)S(1)} %bitcast.170, ...), kind=kOutput, calls=%fused_computation.14.clone.1 | convolution fusion | flops 750489600 | bytes 3457176 | tf_op jit(solution)/shard_map/while/body/eval_jaxpr/hc,hp->cp/dot_general | solution.py:66
  128.1 2.8 %copy.42 = bf16[150,16,256]{2,0,1:T(8,128)(2,1)} copy(bf16[150,16,256]{2,1,0:T(8,128)(2,1)} %get-tuple-element.144) | data formatting | bytes 2457600 | tf_op jit(solution)/shard_map/while | solution.py:106
  131.0 3.8 %all-to-all-start = ((bf16[150,16,256]{2,0,1:T(8,128)(2,1)}), bf16[150,16,256]{2,0,1:T(8,128)(2,1)S(1)}, u32[]{:S(2)}, u32[]{:S(2)}) async-start(bf16[150,16,256]{2,0,1:T(8,128)(2,1)} %copy.42), calls=%async_computation | async-start | bytes 2490368 | tf_op jit(solution)/shard_map/all_to_all | solution.py:109
  135.3 9.3 %multiply_convert_fusion.3 = (bf16[1024,512]{1,0:T(8,128)(2,1)}, bf16[1024,512]{1,0:T(8,128)(2,1)}) fusion(), kind=kLoop, calls=%fused_computation.55 | loop fusion | flops 9961472 | bytes 2097152 | tf_op jit(solution)/shard_map/convert.7
  144.6 6.4 %all-to-all-done = bf16[150,16,256]{2,0,1:T(8,128)(2,1)S(1)} async-done(((bf16[150,16,256]{2,0,1:T(8,128)(2,1)}), bf16[150,16,256]{2,0,1:T(8,128)(2,1)S(1)}, u32[]{:S(2)}, u32[]{:S(2)}) %all-to-all-start) | async-done | bytes 1228832 | tf_op jit(solution)/shard_map/all_to_all | solution.py:109
  152.8 3.0 %fusion.35 = f32[150,4,1024]{2,0,1:T(8,128)S(1)} fusion(bf16[150,4,1024]{2,0,1:T(8,128)(2,1)S(1)} %dot_general.27, bf16[1024,512]{1,0:T(8,128)(2,1)} %get-tuple-element.254, bf16[1024,512]{1,0:T(8,128)(2,1)} %get-tuple-element.255), kind=kOutput, calls=%fused_computation.61 | convolution fusion | flops 1262485504 | bytes 5783552 | tf_op jit(solution)/shard_map/dot_general | solution.py:112
  159.1 1.5 copy.45
  160.6 4.3 %all-to-all-start.1 = ((bf16[4,150,4,256]{3,2,1,0:T(4,128)(2,1)}), bf16[4,150,4,256]{3,2,1,0:T(4,128)(2,1)}, u32[]{:S(2)}, u32[]{:S(2)}) async-start(bf16[4,150,4,256]{3,2,1,0:T(4,128)(2,1)} %copy.45), calls=%async_computation.1 | async-start | bytes 2457600 | tf_op jit(solution)/shard_map/all_to_all | solution.py:124
  165.3 2.0 %copy.56 = f32[19,8,16,256]{3,1,2,0:T(8,128)S(1)} copy(f32[19,8,16,256]{3,2,1,0:T(8,128)S(1)} %bitcast.165) | data formatting | bytes 4980736
  167.3 14.0 %all-to-all-done.1 = bf16[4,150,4,256]{3,2,1,0:T(4,128)(2,1)} async-done(((bf16[4,150,4,256]{3,2,1,0:T(4,128)(2,1)}), bf16[4,150,4,256]{3,2,1,0:T(4,128)(2,1)}, u32[]{:S(2)}, u32[]{:S(2)}) %all-to-all-start.1) | async-done | bytes 1228832 | tf_op jit(solution)/shard_map/all_to_all | solution.py:124
  181.3 2.7 %copy.46 = bf16[150,4,4,256]{3,2,1,0:T(4,128)(2,1)} copy(bf16[150,4,4,256]{3,2,0,1:T(4,128)(2,1)} %bitcast.61) | data formatting | bytes 2457600 | tf_op jit(solution)/shard_map/reshape | solution.py:123
  184.1 3.6 %reshape_reshape.3 = bf16[150,4096]{1,0:T(8,128)(2,1)} reshape(bf16[150,4,4,256]{3,2,1,0:T(4,128)(2,1)} %copy.46) | data formatting | bytes 2457600 | tf_op jit(solution)/shard_map/reshape;reshape | solution.py:128
  187.6 1.9 fusion.24
  (162 shorter events, 29.2 us)
Async XLA Ops:
  0.0 187.6 %copy-start = (bf16[150,150]{1,0:T(8,128)(2,1)S(1)}, bf16[150,150]{1,0:T(8,128)(2,1)}, u32[]{:S(2)}) copy-start(bf16[150,150]{1,0:T(8,128)(2,1)} %param.19) | copy-start | bytes 135004
  0.9 9.1 %copy-start.6 = (f32[150,7,7]{0,2,1:T(8,128)S(1)}, f32[150,7,7]{0,2,1:T(8,128)}, u32[]{:S(2)}) copy-start(f32[150,7,7]{0,2,1:T(8,128)} %param.14) | copy-start | bytes 88204
  5.4 16.8 %copy-start.1 = (s32[1024]{0:T(1024)S(1)}, s32[1024]{0:T(1024)}, u32[]{:S(2)}) copy-start(s32[1024]{0:T(1024)} %param.13) | copy-start | bytes 12292
  8.0 16.6 %collective-permute-start = (bf16[150,16,3]{0,1,2:T(8,128)(2,1)}, bf16[150,16,3]{0,1,2:T(8,128)(2,1)S(1)}, u32[]{:S(2)}, u32[]{:S(2)}) collective-permute-start(bf16[150,16,3]{0,1,2:T(8,128)(2,1)} %get-tuple-element.197), channel_id=1, source_target_pairs={{0,1},{1,2},{2,3},{3,0},{4,5},{5,6},{6,7},{7,4},{8,9},{9,10},{10,1... | collective-permute-start | bytes 43208 | tf_op jit(solution)/shard_map/ppermute | solution.py:16
  8.0 16.6 %collective-permute-start.1 = (bf16[150,16,3]{0,1,2:T(8,128)(2,1)}, bf16[150,16,3]{0,1,2:T(8,128)(2,1)S(1)}, u32[]{:S(2)}, u32[]{:S(2)}) collective-permute-start(bf16[150,16,3]{0,1,2:T(8,128)(2,1)} %get-tuple-element.198), channel_id=1, source_target_pairs={{1,0},{2,1},{3,2},{0,3},{5,4},{6,5},{7,6},{4,7},{9,8},{10,9},{11,1... | collective-permute-start | bytes 43208 | tf_op jit(solution)/shard_map/ppermute | solution.py:18
  27.4 19.8 %collective-permute-start.3 = (bf16[150,3,262]{2,0,1:T(8,128)(2,1)S(1)}, bf16[150,3,262]{2,0,1:T(8,128)(2,1)}, u32[]{:S(2)}, u32[]{:S(2)}) collective-permute-start(bf16[150,3,262]{2,0,1:T(8,128)(2,1)S(1)} %copy.37), channel_id=1, source_target_pairs={{4,0},{8,4},{12,8},{16,12},{20,16},{24,20},{28,24},{5,1},{9,5},{13... | collective-permute-start | bytes 707408 | tf_op jit(solution)/shard_map/ppermute | solution.py:18
  30.7 17.9 %copy-start.46 = (pred[262]{0:T(512)(128)(4,1)S(1)}, pred[262]{0:T(512)(128)(4,1)}, u32[]{:S(2)}) copy-start(pred[262]{0:T(512)(128)(4,1)} %compare_and_fusion) | copy-start | bytes 790
  43.8 13.3 %collective-permute-start.2 = (bf16[150,3,262]{2,0,1:T(8,128)(2,1)}, bf16[150,3,262]{2,0,1:T(8,128)(2,1)}, u32[]{:S(2)}, u32[]{:S(2)}) collective-permute-start(bf16[150,3,262]{2,0,1:T(8,128)(2,1)} %copy.33), channel_id=1, source_target_pairs={{0,4},{4,8},{8,12},{12,16},{16,20},{20,24},{24,28},{1,5},{5,9},{9,... | collective-permute-start | bytes 707408 | tf_op jit(solution)/shard_map/ppermute | solution.py:16
  58.4 5.5 %copy-start.7 = (f32[150,1,1]{0,2,1:T(1,128)S(1)}, f32[150,1,1]{0,2,1:T(1,128)}, u32[]{:S(2)}) copy-start(f32[150,1,1]{0,2,1:T(1,128)} %get-tuple-element.227) | copy-start | bytes 1804
  58.4 5.5 %copy-start.8 = (f32[150,1,1]{0,2,1:T(1,128)S(1)}, f32[150,1,1]{0,2,1:T(1,128)}, u32[]{:S(2)}) copy-start(f32[150,1,1]{0,2,1:T(1,128)} %get-tuple-element.228) | copy-start | bytes 1804
  58.4 5.5 %copy-start.9 = (f32[150,1,1]{0,2,1:T(1,128)S(1)}, f32[150,1,1]{0,2,1:T(1,128)}, u32[]{:S(2)}) copy-start(f32[150,1,1]{0,2,1:T(1,128)} %get-tuple-element.229) | copy-start | bytes 1804
  58.5 5.5 %copy-start.10 = (f32[150,1,1]{0,2,1:T(1,128)S(1)}, f32[150,1,1]{0,2,1:T(1,128)}, u32[]{:S(2)}) copy-start(f32[150,1,1]{0,2,1:T(1,128)} %get-tuple-element.230) | copy-start | bytes 1804
  58.5 5.5 %copy-start.11 = (f32[150,1,1]{0,2,1:T(1,128)S(1)}, f32[150,1,1]{0,2,1:T(1,128)}, u32[]{:S(2)}) copy-start(f32[150,1,1]{0,2,1:T(1,128)} %get-tuple-element.231) | copy-start | bytes 1804
  58.5 5.5 %copy-start.12 = (f32[150,1,1]{0,2,1:T(1,128)S(1)}, f32[150,1,1]{0,2,1:T(1,128)}, u32[]{:S(2)}) copy-start(f32[150,1,1]{0,2,1:T(1,128)} %get-tuple-element.232) | copy-start | bytes 1804
  58.5 5.5 %copy-start.13 = (f32[150,1,1]{0,2,1:T(1,128)S(1)}, f32[150,1,1]{0,2,1:T(1,128)}, u32[]{:S(2)}) copy-start(f32[150,1,1]{0,2,1:T(1,128)} %get-tuple-element.233) | copy-start | bytes 1804
  58.5 5.5 %copy-start.14 = (f32[150,1,1]{0,2,1:T(1,128)S(1)}, f32[150,1,1]{0,2,1:T(1,128)}, u32[]{:S(2)}) copy-start(f32[150,1,1]{0,2,1:T(1,128)} %get-tuple-element.234) | copy-start | bytes 1804
  58.5 5.5 %copy-start.15 = (f32[150,1,1]{0,2,1:T(1,128)S(1)}, f32[150,1,1]{0,2,1:T(1,128)}, u32[]{:S(2)}) copy-start(f32[150,1,1]{0,2,1:T(1,128)} %get-tuple-element.235) | copy-start | bytes 1804
  58.5 5.5 %copy-start.16 = (f32[150,1,1]{0,2,1:T(1,128)S(1)}, f32[150,1,1]{0,2,1:T(1,128)}, u32[]{:S(2)}) copy-start(f32[150,1,1]{0,2,1:T(1,128)} %get-tuple-element.236) | copy-start | bytes 1804
  58.5 5.5 %copy-start.17 = (f32[150,1,1]{0,2,1:T(1,128)S(1)}, f32[150,1,1]{0,2,1:T(1,128)}, u32[]{:S(2)}) copy-start(f32[150,1,1]{0,2,1:T(1,128)} %get-tuple-element.237) | copy-start | bytes 1804
  58.5 5.5 %copy-start.18 = (f32[150,1,1]{0,2,1:T(1,128)S(1)}, f32[150,1,1]{0,2,1:T(1,128)}, u32[]{:S(2)}) copy-start(f32[150,1,1]{0,2,1:T(1,128)} %get-tuple-element.238) | copy-start | bytes 1804
  58.5 5.5 %copy-start.19 = (f32[150,1,1]{0,2,1:T(1,128)S(1)}, f32[150,1,1]{0,2,1:T(1,128)}, u32[]{:S(2)}) copy-start(f32[150,1,1]{0,2,1:T(1,128)} %get-tuple-element.239) | copy-start | bytes 1804
  58.5 5.5 %copy-start.20 = (f32[150,1,1]{0,2,1:T(1,128)S(1)}, f32[150,1,1]{0,2,1:T(1,128)}, u32[]{:S(2)}) copy-start(f32[150,1,1]{0,2,1:T(1,128)} %get-tuple-element.240) | copy-start | bytes 1804
  58.6 5.5 %copy-start.21 = (f32[150,1,1]{0,2,1:T(1,128)S(1)}, f32[150,1,1]{0,2,1:T(1,128)}, u32[]{:S(2)}) copy-start(f32[150,1,1]{0,2,1:T(1,128)} %get-tuple-element.241) | copy-start | bytes 1804
  58.6 5.5 %copy-start.22 = (f32[150,1,1]{0,2,1:T(1,128)S(1)}, f32[150,1,1]{0,2,1:T(1,128)}, u32[]{:S(2)}) copy-start(f32[150,1,1]{0,2,1:T(1,128)} %get-tuple-element.242) | copy-start | bytes 1804
  58.6 5.5 %copy-start.23 = (f32[150,1,1]{0,2,1:T(1,128)S(1)}, f32[150,1,1]{0,2,1:T(1,128)}, u32[]{:S(2)}) copy-start(f32[150,1,1]{0,2,1:T(1,128)} %get-tuple-element.243) | copy-start | bytes 1804
  58.6 5.5 %copy-start.24 = (f32[150,1,1]{0,2,1:T(1,128)S(1)}, f32[150,1,1]{0,2,1:T(1,128)}, u32[]{:S(2)}) copy-start(f32[150,1,1]{0,2,1:T(1,128)} %get-tuple-element.244) | copy-start | bytes 1804
  105.6 6.3 %copy-start.47 = (bf16[150,600]{1,0:T(8,128)(2,1)S(1)}, bf16[150,600]{1,0:T(8,128)(2,1)}, u32[]{:S(2)}) copy-start(bf16[150,600]{1,0:T(8,128)(2,1)} %param.16) | copy-start | bytes 540004
  105.6 6.3 %copy-start.48 = (f32[150]{0:T(256)S(1)}, f32[150]{0:T(256)}, u32[]{:S(2)}) copy-start(f32[150]{0:T(256)} %param.15) | copy-start | bytes 1804
  128.1 6.6 %copy-start.5 = (f32[2,150,512]{2,0,1:T(2,128)S(1)}, f32[2,150,512]{2,0,1:T(2,128)}, u32[]{:S(2)}) copy-start(f32[2,150,512]{2,0,1:T(2,128)} %param.18) | copy-start | bytes 1843204
  131.0 20.0 %all-to-all-start = ((bf16[150,16,256]{2,0,1:T(8,128)(2,1)}), bf16[150,16,256]{2,0,1:T(8,128)(2,1)S(1)}, u32[]{:S(2)}, u32[]{:S(2)}) async-start(bf16[150,16,256]{2,0,1:T(8,128)(2,1)} %copy.42), calls=%async_computation | async-start | bytes 2490368 | tf_op jit(solution)/shard_map/all_to_all | solution.py:109
  158.9 6.0 %copy-start.2 = (bf16[150,16,256]{2,1,0:T(8,128)(2,1)S(1)}, bf16[150,16,256]{2,1,0:T(8,128)(2,1)}, u32[]{:S(2)}) copy-start(bf16[150,16,256]{2,1,0:T(8,128)(2,1)} %get-tuple-element.144) | copy-start | bytes 3686404
  160.6 20.7 %all-to-all-start.1 = ((bf16[4,150,4,256]{3,2,1,0:T(4,128)(2,1)}), bf16[4,150,4,256]{3,2,1,0:T(4,128)(2,1)}, u32[]{:S(2)}, u32[]{:S(2)}) async-start(bf16[4,150,4,256]{3,2,1,0:T(4,128)(2,1)} %copy.45), calls=%async_computation.1 | async-start | bytes 2457600 | tf_op jit(solution)/shard_map/all_to_all | solution.py:124
  (23 other events, 118.4 us)
